TPU v7x, 32 devices: a whole 2x2x4 slice. The times are simulated.
32 devices in a mesh: tok: 4 (over x, core), exp: 8 (over z, y).
Axes of the slice: x: 2, y: 2, z: 4, core: 2. Of those that a mesh axis runs over, the one named last changes fastest.
Arguments:
- tokens: bfloat16 [8, 1024, 1024], P('exp', 'tok'), may hold values from -6 to 6
- upstream: bfloat16 [8, 1024, 1024], P('exp', 'tok'), may hold values from -6 to 6
- dispatch: bfloat16 [8, 1024, 8], P('exp', 'tok'), may hold values from 0 to 1, as said below
- combine: bfloat16 [8, 1024, 8], P('exp', 'tok'), may hold values from 0 to 1, as said below
- w_in: bfloat16 [8, 1024, 2048], P('exp', None, 'tok'), may hold values from -0.1875 to 0.1875
- w_out: bfloat16 [8, 2048, 1024], P('exp', 'tok'), may hold values from -0.125 to 0.125
- slot_keys: bfloat16 [1024, 8], replicated, may hold values from -0.1875 to 0.1875
Outputs:
- token_grad: bfloat16 [8, 1024, 1024], P('exp', 'tok')
Inputs may be any that keep to these rules, and one draw needn't show every extreme that they name: `dispatch`: for each image and slot the entries over the image's tokens are positive and sum to one up to rounding. `combine`: for each token the entries over the 8 slots are positive and sum to one up to rounding.
All inputs are finite; a program needn't handle non-finite values.
Results may differ from a plain program's by a relative error of at most 0.025.
Values may be sent and summed in bfloat16 or wider, within the bound.
A program may use at most 64 MiB of HBM per device.

v0:
```python
import functools

import jax
import jax.numpy as jnp
from jax import lax
from jax.experimental import pallas as pl
from jax.experimental.pallas import tpu as pltpu
from jax.sharding import PartitionSpec as P

MESH = pl.DeviceIdType.MESH
LANES = 128
NT = (((1,), (1,)), ((), ()))
NN = (((1,), (0,)), ((), ()))
TN = (((0,), (0,)), ((), ()))


def gelu_parts(pre_act):
    inside = 0.7978845608 * (pre_act + 0.044715 * pre_act * pre_act * pre_act)
    tanh_val = jnp.tanh(inside)
    gelu_value = 0.5 * pre_act * (1.0 + tanh_val)
    gelu_slope = 0.5 * (1.0 + tanh_val) + 0.5 * pre_act * (
        1.0 - tanh_val * tanh_val
    ) * 0.7978845608 * (1.0 + 3.0 * 0.044715 * pre_act * pre_act)
    return (gelu_value, gelu_slope)


def mm(a, b, dims):
    return lax.dot_general(a, b, dims, preferred_element_type=jnp.float32)


def partner(me, k, count):
    if count & (count - 1):
        return lax.rem(me + k, count)
    for bit in range(count.bit_length() - 1):
        if k >> bit & 1:
            me = me + (1 << bit) * (1 - 2 * (me // (1 << bit) % 2))
    return me


def kernel(
    n_tok, n_exp,
    tok_hbm, up_hbm, disp_hbm, comb_hbm, win_hbm, wout_hbm, keys_hbm,
    left_ref, right_ref,
    tok, up, disp, comb, win, wout, keys, tok_t, up_t, win_t, wout_t,
    rows, send1, recv1, send2, recv2, part, parts,
    load_sem, send_sem, recv_sem,
):
    t_me, e_me = lax.axis_index("tok"), lax.axis_index("exp")
    me = t_me * n_exp + e_me
    n_dev = n_tok * n_exp
    width = tok.shape[1]
    chunks = width // LANES

    loads = [
        pltpu.make_async_copy(src, dst, load_sem.at[k])
        for k, (src, dst) in enumerate((
            (disp_hbm, disp), (tok_hbm, tok), (comb_hbm, comb), (up_hbm, up),
            (win_hbm, win), (wout_hbm, wout), (keys_hbm, keys),
        ))
    ]

    barrier = pltpu.get_barrier_semaphore()

    def others(act):
        if n_exp <= 16:
            for dt in reversed(range(n_tok)):
                for k in reversed(range(n_exp)):
                    if k or dt:
                        act(partner(t_me, dt, n_tok), partner(e_me, k, n_exp))
            return

        @pl.loop(0, n_exp)
        def _(k):
            e = lax.rem(e_me + k, n_exp)
            for dt in range(1, n_tok):
                act(lax.rem(t_me + dt, n_tok), e)
            pl.when(k > 0)(functools.partial(act, t_me, e))

    others(lambda t, e: pl.semaphore_signal(
        barrier, inc=1, device_id=(t, e), device_id_type=MESH))
    for copy in loads:
        copy.start()

    def spread(first, second):
        for j in range(chunks):
            cut = slice(j * LANES, (j + 1) * LANES)
            rows[pl.ds(j, n_exp, stride=2 * chunks), :] = first[:, cut]
            rows[pl.ds(chunks + j, n_exp, stride=2 * chunks), :] = second[:, cut]
        return rows[...].reshape(n_exp, 2 * chunks, LANES).astype(jnp.bfloat16)

    def gather(which):
        return jnp.concatenate(
            [rows[pl.ds(which * chunks + j, n_exp, stride=2 * chunks), :] for j in range(chunks)],
            axis=1,
        )

    def exchange(send, recv, way):
        def act(t, e):
            pltpu.make_async_remote_copy(
                src_ref=send.at[e], dst_ref=recv.at[me],
                send_sem=send_sem.at[way], recv_sem=recv_sem.at[way],
                device_id=(t, e), device_id_type=MESH,
            ).start()
        others(act)

    def arrived(recv, way):
        some = recv.at[pl.ds(0, n_dev - 1)]
        pltpu.make_async_copy(some, some, recv_sem.at[way]).wait()
        total = jnp.zeros((n_exp, 2 * chunks, LANES), jnp.float32)
        for t in range(n_tok):
            total = total + recv[pl.ds(t * n_exp, n_exp)].astype(jnp.float32)
        rows[...] = total.reshape(n_exp * 2 * chunks, LANES)
        return gather(0).astype(jnp.bfloat16), gather(1).astype(jnp.bfloat16)

    loads[0].wait()
    loads[1].wait()
    slot_in = mm(disp[...], tok[...], NN)
    loads[2].wait()
    loads[3].wait()
    slot_grad = mm(comb[...], up[...], NN)
    slabs = spread(slot_in, slot_grad)
    send1[...] = slabs
    recv1[me] = send1[e_me]
    part[...] = slot_in.astype(jnp.bfloat16)
    parts[t_me] = part[...]
    pl.semaphore_wait(barrier, n_dev - 1)
    exchange(send1, recv1, 0)
    for dt in range(1, n_tok):
        pltpu.make_async_remote_copy(
            src_ref=part, dst_ref=parts.at[t_me],
            send_sem=send_sem.at[2], recv_sem=recv_sem.at[2],
            device_id=(lax.rem(t_me + dt, n_tok), e_me), device_id_type=MESH,
        ).start()
    loads[4].wait()
    loads[5].wait()
    loads[6].wait()
    wout_t[...] = wout[...].T
    win_t[...] = win[...].T

    in_rows, grad_rows = arrived(recv1, 0)
    pre_act = mm(in_rows, win[...], NN)
    hidden_grad = mm(grad_rows, wout_t[...], NN)
    gelu_value, gelu_slope = gelu_parts(pre_act)
    slot_out = mm(gelu_value.astype(jnp.bfloat16), wout[...], NN)
    slot_back = mm((hidden_grad * gelu_slope).astype(jnp.bfloat16), win_t[...], NN)
    send2[...] = spread(slot_out, slot_back)
    recv2[me] = send2[e_me]
    exchange(send2, recv2, 1)

    some = parts.at[pl.ds(0, n_tok - 1)]
    pltpu.make_async_copy(some, some, recv_sem.at[2]).wait()
    tok_t[...] = tok[...].T
    up_t[...] = up[...].T
    in_total = parts[0].astype(jnp.float32)
    for t in range(1, n_tok):
        in_total = in_total + parts[t].astype(jnp.float32)

    out_rows, back_rows = arrived(recv2, 1)
    comb_grad = mm(out_rows, up_t[...], NN)
    disp_grad = mm(back_rows, tok_t[...], NN)
    totals = jnp.sum(in_total * back_rows.astype(jnp.float32), axis=1, keepdims=True)
    comb_full = comb[...].astype(jnp.float32)
    disp_full = disp[...].astype(jnp.float32)
    comb_logit = comb_full * (comb_grad - jnp.sum(comb_full * comb_grad, axis=0, keepdims=True))
    logit_grad = comb_logit + disp_full * (disp_grad - totals)
    left = jnp.concatenate([disp_full, logit_grad], axis=0).astype(jnp.bfloat16)
    right = jnp.concatenate(
        [back_rows.astype(jnp.float32), keys[...].astype(jnp.float32)], axis=0
    ).astype(jnp.bfloat16)
    left_ref[...] = left
    right_ref[...] = right

    for way, sent in enumerate((recv1.at[pl.ds(0, n_dev - 1)], recv2.at[pl.ds(0, n_dev - 1)], some)):
        pltpu.make_async_copy(sent, sent, send_sem.at[way]).wait()


def finish(left, right, out_hbm, held, sem):
    pieces = 4
    count = held.shape[0] // pieces
    copies = []
    for k in range(pieces):
        cut = slice(k * count, (k + 1) * count)
        held[cut] = mm(left[:, cut], right[...], TN).astype(jnp.bfloat16)
        copies.append(pltpu.make_async_copy(held.at[cut], out_hbm.at[cut], sem.at[k]))
        copies[-1].start()
    for copy in copies:
        copy.wait()


def solution(mesh):
    n_tok, n_exp = mesh.shape["tok"], mesh.shape["exp"]

    def body(tokens, upstream, dispatch, combine, w_in, w_out, slot_keys):
        args = (
            tokens[0], upstream[0], dispatch[0].T, combine[0].T, w_in[0], w_out[0], slot_keys.T,
        )
        count, width = args[0].shape
        slab = (2 * width // LANES, LANES)
        bf16 = jnp.bfloat16
        left, right = pl.pallas_call(
            functools.partial(kernel, n_tok, n_exp),
            out_shape=(jax.ShapeDtypeStruct((2 * n_exp, count), bf16), jax.ShapeDtypeStruct((2 * n_exp, width), bf16)),
            in_specs=[pl.BlockSpec(memory_space=pltpu.HBM)] * len(args),
            out_specs=(pl.BlockSpec(memory_space=pltpu.VMEM),) * 2,
            scratch_shapes=[pltpu.VMEM(a.shape, bf16) for a in args] + [
                pltpu.VMEM(args[k].shape[::-1], bf16) for k in (0, 1, 4, 5)
            ] + [
                pltpu.VMEM((n_exp * slab[0], LANES), jnp.float32),
                pltpu.VMEM((n_exp,) + slab, bf16),
                pltpu.VMEM((n_tok * n_exp,) + slab, bf16),
                pltpu.VMEM((n_exp,) + slab, bf16),
                pltpu.VMEM((n_tok * n_exp,) + slab, bf16),
                pltpu.VMEM((n_exp, width), bf16),
                pltpu.VMEM((n_tok, n_exp, width), bf16),
                pltpu.SemaphoreType.DMA((len(args),)),
                pltpu.SemaphoreType.DMA((3,)),
                pltpu.SemaphoreType.DMA((3,)),
            ],
            compiler_params=pltpu.CompilerParams(
                collective_id=0, has_side_effects=True, vmem_limit_bytes=40 << 20
            ),
            name="soft_moe_back",
        )(*[pltpu.with_memory_space_constraint(a, pltpu.HBM) for a in args])
        result = pl.pallas_call(
            finish,
            out_shape=jax.ShapeDtypeStruct((count, width), bf16),
            in_specs=[pl.BlockSpec(memory_space=pltpu.VMEM)] * 2,
            out_specs=pl.BlockSpec(memory_space=pltpu.HBM),
            scratch_shapes=[pltpu.VMEM((count, width), bf16), pltpu.SemaphoreType.DMA((4,))],
            compiler_params=pltpu.CompilerParams(vmem_limit_bytes=4 << 20),
            name="finish",
        )(left, right)
        return result[None]

    placed = (
        P("exp", "tok", None),
        P("exp", "tok", None),
        P("exp", "tok", None),
        P("exp", "tok", None),
        P("exp", None, "tok"),
        P("exp", "tok", None),
        P(),
    )
    return jax.shard_map(
        body, mesh=mesh, in_specs=placed, out_specs=P("exp", "tok", None), check_vma=False
    )
```

profile of v0, /device:TPU:0, one launch (start us, length us, event | category | flops | bytes accessed | tf_op | source)
XLA Modules:
  0.0 19.2 jit_solution(7797719644294937944)
XLA Ops:
  0.0 18.1 %soft_moe_back.1 = (bf16[16,256]{1,0:T(8,128)(2,1)S(1)}, bf16[16,1024]{1,0:T(8,128)(2,1)S(1)}) custom-call(bf16[256,1024]{1,0:T(8,128)(2,1)} %bitcast.14, bf16[256,1024]{1,0:T(8,128)(2,1)} %bitcast.15, bf16[8,256]{1,0:T(8,128)(2,1)} %bitcast.17, bf16[8,256]{1,0:T(8,128)(2,1)} %bitcast.18, bf16[1024,512]{1,0:T(8,128)(2,1)} %bitcast.12, ...), custom_call_target="tpu_custom_call" | custom-call | tf_op jit(solution)/shard_map/soft_moe_back/pallas_call | solution.py:200
  18.2 1.1 %finish.1 = bf16[256,1024]{1,0:T(8,128)(2,1)} custom-call(bf16[16,256]{1,0:T(8,128)(2,1)S(1)} %get-tuple-element.7.left, bf16[16,1024]{1,0:T(8,128)(2,1)S(1)} %get-tuple-element.8.right), custom_call_target="tpu_custom_call" | custom-call | tf_op jit(solution)/shard_map/finish/pallas_call | solution.py:224
where the time goes:
time: 19.4 us; the launch traced here: 19.2 us
  Pallas kernels  19.2 us (99%)
    pallas_call x1, Pallas kernels, body(): pl.pallas_call(functools.partial(kernel, n_tok, n_exp), out_shape=(jax.Sh...  18.1 us
    pallas_call x1, Pallas kernels, body(): pl.pallas_call(finish, out_shape=jax.ShapeDtypeStruct((count, width), bf1...  1.05 us

commit v1 on v0

--- a/solution.py
+++ b/solution.py
@@ -94,6 +94,11 @@
             axis=1,
         )
 
+    def towards(act):
+        dests = [(t, e) for t in range(n_tok) for e in range(n_exp)]
+        for t, e in sorted(dests, key=lambda d: bin(d[0] >> 1).count("1") + d[1] // 2 + d[1] % 2):
+            pl.when((t_me != t) | (e_me != e))(functools.partial(act, t, e))
+
     def exchange(send, recv, way):
         def act(t, e):
             pltpu.make_async_remote_copy(
@@ -101,7 +106,10 @@
                 send_sem=send_sem.at[way], recv_sem=recv_sem.at[way],
                 device_id=(t, e), device_id_type=MESH,
             ).start()
-        others(act)
+        if way and n_exp <= 16:
+            towards(act)
+        else:
+            others(act)
 
     def arrived(recv, way):
         some = recv.at[pl.ds(0, n_dev - 1)]

time: 19.4 us -> 18.6 us (0.959)
  Pallas kernels: 19.2 us -> 18.5 us
    pallas_call x1, Pallas kernels: 18.1 us -> 17.4 us  [body(): pl.pallas_call(functools.partial(kernel, n_tok, n_exp), out_shape=(jax.Sh...]
where the time goes in v1:
time: 18.6 us; the launch traced here: 18.5 us
  Pallas kernels  18.5 us (99%)
    pallas_call x1, Pallas kernels, body(): pl.pallas_call(functools.partial(kernel, n_tok, n_exp), out_shape=(jax.Sh...  17.4 us
    pallas_call x1, Pallas kernels, body(): pl.pallas_call(finish, out_shape=jax.ShapeDtypeStruct((count, width), bf1...  1.05 us

profile of v1, /device:TPU:0, one launch (start us, length us, event | category | flops | bytes accessed | tf_op | source)
XLA Modules:
  0.0 18.5 jit_solution(13387644802954472118)
XLA Ops:
  0.0 17.4 %soft_moe_back.1 = (bf16[16,256]{1,0:T(8,128)(2,1)S(1)}, bf16[16,1024]{1,0:T(8,128)(2,1)S(1)}) custom-call(bf16[256,1024]{1,0:T(8,128)(2,1)} %bitcast.14, bf16[256,1024]{1,0:T(8,128)(2,1)} %bitcast.15, bf16[8,256]{1,0:T(8,128)(2,1)} %bitcast.17, bf16[8,256]{1,0:T(8,128)(2,1)} %bitcast.18, bf16[1024,512]{1,0:T(8,128)(2,1)} %bitcast.12, ...), custom_call_target="tpu_custom_call" | custom-call | tf_op jit(solution)/shard_map/soft_moe_back/pallas_call | solution.py:208
  17.4 1.1 %finish.1 = bf16[256,1024]{1,0:T(8,128)(2,1)} custom-call(bf16[16,256]{1,0:T(8,128)(2,1)S(1)} %get-tuple-element.7.left, bf16[16,1024]{1,0:T(8,128)(2,1)S(1)} %get-tuple-element.8.right), custom_call_target="tpu_custom_call" | custom-call | tf_op jit(solution)/shard_map/finish/pallas_call | solution.py:232
